TPU v7x, 32 devices: a whole 2x2x4 slice. The times are simulated.
32 devices in a mesh: gx: 4 (over z), wa: 8 (over y, x, core).
Axes of the slice: x: 2, y: 2, z: 4, core: 2. Of those that a mesh axis runs over, the one named last changes fastest.
Arguments:
- positions: float32 [512, 3, 256], P(('gx', 'wa')), may hold values from 0 to 1
- weights: float32 [512, 256], P(('gx', 'wa')), may hold values from 0.5 to 2
- block_count: int32 [512], P(('gx', 'wa')), may hold values from 1 to 256
- send_list: int32 [32, 8, 2], P(('gx', 'wa')), may hold values from 0 to 15
- unit_pair: int32 [32, 16], P(('gx', 'wa')), may hold values from 0 to 15, each once within a row
- unit_live: int32 [32], P(('gx', 'wa')), may hold values from 2 to 16, as said below
Outputs:
- slab_counts: float32 [4, 30, 20], P('gx')
- totals: float32 [30, 20], replicated
Inputs may be any that keep to these rules, and one draw needn't show every extreme that they name: `unit_pair`: each row holds every slot number once. `unit_live`: the active units of a device are the first ones of its list; some device has all 16 active.
All inputs are finite; a program needn't handle non-finite values.
Results may differ from a plain program's by a relative error of at most 0.0003.
Values sent between devices are 32-bit elements; how exact they have to be, the bound alone decides.
No kernel may reach another device: no remote copies, remote signals or barrier semaphores. Data moves between devices by JAX's collectives and lax.ppermute only.
A program may use at most 64 MiB of HBM per device.

v0:
```python
import jax
import jax.numpy as jnp
from jax import lax
from jax.sharding import PartitionSpec as P

SBINS = 30
MUBINS = 20
reach = 0.5
viewer = (0.5, 0.5, -1.5)
units_per_turn = 4


def passed_along(shard, axis, by):
    count = lax.axis_size(axis)
    return lax.ppermute(shard, axis, [(i, (i + by) % count) for i in range(count)])


def group_counts(a_pos, a_wgt, b_pos, b_wgt):
    step = reach / SBINS
    diff = a_pos[:, :, :, None] - b_pos[:, :, None, :]
    eye_at = jnp.array(viewer, dtype=jnp.float32)[None, :, None, None]
    middle = 0.5 * (a_pos[:, :, :, None] + b_pos[:, :, None, :]) + eye_at
    square = jnp.sum(diff * diff, axis=1)
    dist = jnp.sqrt(square)
    along = jnp.abs(jnp.sum(diff * middle, axis=1)) / jnp.sqrt(
        jnp.maximum(square, step * step) * jnp.sum(middle * middle, axis=1)
    )
    s_mid = jnp.arange(SBINS, dtype=jnp.float32) + 0.5
    m_mid = jnp.arange(MUBINS, dtype=jnp.float32) + 0.5
    s_hat = jnp.maximum(
        0.0, 1.0 - jnp.abs(dist[:, None] / step - s_mid[None, :, None, None])
    ).astype(jnp.bfloat16)
    pair_w = a_wgt[:, :, None] * b_wgt[:, None, :]
    m_hat = (
        jnp.maximum(0.0, 1.0 - jnp.abs(along[:, None] * MUBINS - m_mid[None, :, None, None]))
        * pair_w[:, None]
    ).astype(jnp.bfloat16)
    return jnp.einsum("gkab,gjab->kj", s_hat, m_hat, preferred_element_type=jnp.float32)


def per_device(positions, weights, block_count, send_list, unit_pair, unit_live):
    block = positions.shape[2]
    per_peer = send_list.shape[2]
    peers = lax.axis_size("wa")
    units = peers * per_peer
    live = jnp.arange(block, dtype=jnp.int32)[None, :] < block_count[:, None]
    masked = jnp.where(live, weights, jnp.float32(0.0))
    picks = send_list[0].reshape(-1)
    send_pos = positions[picks].reshape(peers, per_peer, 3, block)
    send_wgt = masked[picks].reshape(peers, per_peer, block)
    own_pos, own_wgt = (
        lax.all_to_all(send_pos, "wa", split_axis=0, concat_axis=0, tiled=True),
        lax.all_to_all(send_wgt, "wa", split_axis=0, concat_axis=0, tiled=True),
    )
    below_pos, below_wgt = passed_along((own_pos, own_wgt), "gx", 1)
    own_pos = own_pos.reshape(units, 3, block)
    own_wgt = own_wgt.reshape(units, block)
    below_pos = below_pos.reshape(units, 3, block)
    below_wgt = below_wgt.reshape(units, block)
    partner = unit_pair[0]
    partner_pos = below_pos[partner]
    partner_wgt = below_wgt[partner]
    active = jnp.arange(units, dtype=jnp.int32) < unit_live[0]
    own_wgt = jnp.where(active[:, None], own_wgt, jnp.float32(0.0))
    start = jnp.zeros((SBINS, MUBINS), jnp.float32)
    turns = units // units_per_turn
    items = (
        own_pos.reshape(turns, units_per_turn, 3, block),
        own_wgt.reshape(turns, units_per_turn, block),
        partner_pos.reshape(turns, units_per_turn, 3, block),
        partner_wgt.reshape(turns, units_per_turn, block),
    )

    def accumulate(total, group):
        return (total + group_counts(*group), None)

    total, _ = lax.scan(accumulate, start, items)
    scale = 10.0 * SBINS * MUBINS / (peers * units * block * block)
    slab = lax.psum(total, "wa") * scale
    whole = lax.psum(slab, "gx") / lax.axis_size("gx")
    return (slab[None], whole)


def solution(mesh):
    return jax.shard_map(
        per_device,
        mesh=mesh,
        in_specs=(
            P(("gx", "wa"), None, None),
            P(("gx", "wa"), None),
            P(("gx", "wa")),
            P(("gx", "wa"), None, None),
            P(("gx", "wa"), None),
            P(("gx", "wa")),
        ),
        out_specs=(P("gx", None, None), P()),
        check_vma=False,
    )
```

profile of v0, /device:TPU:0, one launch (start us, length us, event | category | flops | bytes accessed | tf_op | source)
XLA Modules:
  0.0 132.2 jit_solution(15789836194075726807)
XLA Ops:
  0.6 0.0 copy-start
  0.6 0.0 copy-start.1
  0.7 0.8 copy.30
  1.4 0.1 reshape_squeeze.3
  1.5 0.8 fusion.12
  2.3 0.6 gather_fusion.2
  2.9 0.6 reshape.132
  3.5 5.2 %all-to-all-start.1 = ((f32[8,2,256]{2,1,0:T(2,128)}), f32[8,2,256]{2,1,0:T(2,128)S(1)}, u32[]{:S(2)}, u32[]{:S(2)}) async-start(f32[8,2,256]{2,1,0:T(2,128)} %reshape.132), calls=%async_computation.1 | async-start | bytes 32768 | tf_op jit(solution)/shard_map/all_to_all | solution.py:53
  8.7 0.7 fusion.14
  9.4 0.0 copy-done
  9.4 0.6 gather_fusion
  10.0 0.6 copy.31
  11.3 2.1 %all-to-all-done.1 = f32[8,2,256]{2,1,0:T(2,128)S(1)} async-done(((f32[8,2,256]{2,1,0:T(2,128)}), f32[8,2,256]{2,1,0:T(2,128)S(1)}, u32[]{:S(2)}, u32[]{:S(2)}) %all-to-all-start.1) | async-done | bytes 16416 | tf_op jit(solution)/shard_map/all_to_all | solution.py:53
  13.5 3.3 %all-to-all-start = ((f32[8,2,3,256]{3,1,2,0:T(2,128)}), f32[8,2,3,256]{3,1,2,0:T(2,128)S(1)}, u32[]{:S(2)}, u32[]{:S(2)}) async-start(f32[8,2,3,256]{3,1,2,0:T(2,128)} %copy.31), calls=%async_computation | async-start | bytes 98304 | tf_op jit(solution)/shard_map/all_to_all | solution.py:52
  16.8 1.6 %collective-permute-start.1 = (f32[8,2,256]{2,1,0:T(2,128)S(1)}, f32[8,2,256]{2,1,0:T(2,128)S(1)}, u32[]{:S(2)}, u32[]{:S(2)}) collective-permute-start(f32[8,2,256]{2,1,0:T(2,128)S(1)} %all-to-all-done.1), channel_id=1, source_target_pairs={{0,8},{8,16},{16,24},{24,0},{1,9},{9,17},{17,25},{25,1},{2,10},{10... | collective-permute-start | bytes 49160 | tf_op jit(solution)/shard_map/ppermute | solution.py:15
  18.5 3.2 %all-to-all-done = f32[8,2,3,256]{3,1,2,0:T(2,128)S(1)} async-done(((f32[8,2,3,256]{3,1,2,0:T(2,128)}), f32[8,2,3,256]{3,1,2,0:T(2,128)S(1)}, u32[]{:S(2)}, u32[]{:S(2)}) %all-to-all-start) | async-done | bytes 49184 | tf_op jit(solution)/shard_map/all_to_all | solution.py:52
  21.7 1.6 %collective-permute-start = (f32[8,2,3,256]{3,1,2,0:T(2,128)S(1)}, f32[8,2,3,256]{3,1,2,0:T(2,128)S(1)}, u32[]{:S(2)}, u32[]{:S(2)}) collective-permute-start(f32[8,2,3,256]{3,1,2,0:T(2,128)S(1)} %all-to-all-done), channel_id=1, source_target_pairs={{0,8},{8,16},{16,24},{24,0},{1,9},{9,17},{17,25},{25,1},{2,10},{10... | collective-permute-start | bytes 147464 | tf_op jit(solution)/shard_map/ppermute | solution.py:15
  23.3 0.1 broadcast_select_fusion
  23.3 0.0 collective-permute-done.1
  23.4 0.6 gather_fusion.3
  24.0 3.6 %collective-permute-done = f32[8,2,3,256]{3,1,2,0:T(2,128)S(1)} collective-permute-done((f32[8,2,3,256]{3,1,2,0:T(2,128)S(1)}, f32[8,2,3,256]{3,1,2,0:T(2,128)S(1)}, u32[]{:S(2)}, u32[]{:S(2)}) %collective-permute-start) | collective-permute-done | bytes 49184 | tf_op jit(solution)/shard_map/ppermute | solution.py:15
  27.6 0.6 gather_fusion.1
  28.2 0.0 copy-done.1
  28.2 63.3 %while.12 = (s32[]{:T(128)}, f32[30,20]{0,1:T(8,128)S(1)}, f32[4,4,3,256]{3,2,1,0:T(4,128)S(1)}, f32[4,4,3,256]{3,2,1,0:T(4,128)S(1)}, f32[4,4,256]{2,1,0:T(4,12...) while((s32[]{:T(128)}, f32[30,20]{0,1:T(8,128)S(1)}, ...), condition=%wide.region_4.5_spmd.clone.clone, body=%wide.region_0.4_spmd.sunk.clone.clone.sunk | while | flops 394265856 | bytes 16889040 | solution.py:77
  28.2 1.4 %fusion.17 = (f32[4,256,256]{2,1,0:T(8,128)S(1)}, f32[4,256,256]{2,1,0:T(8,128)S(1)}, f32[4,256,256]{2,1,0:T(8,128)S(1)}) fusion(f32[3]{0:T(128)S(1)} %get-tuple-element.207, f32[4,3,256]{2,1,0:T(4,128)S(1)} %get-tuple-element.175, f32[4,3,256]{2,1,0:T(4,128)S(1)} %get-tuple-element.176), kind=kLoop, calls=%fused_computation.15.clone.1 | loop fusion | flops 7077888 | bytes 3170316 | tf_op jit(solution)/shard_map/while/body/eval_jaxpr/reduce_sum | solution.py:25
  29.7 0.5 sqrt_multiply_fusion.2
  30.2 0.7 copy.44
  30.8 0.7 copy.45
  31.5 0.1 copy.43
  31.7 0.3 broadcast_multiply_fusion.4
  32.1 11.9 %fusion.18 = f32[30,20]{0,1:T(8,128)S(1)} fusion(f32[4,256,256]{2,0,1:T(4,128)S(1)} %broadcast_multiply_fusion.4, f32[20]{0:T(128)S(1)} %iota_add_fusion.4, f32[4,256,256]{2,0,1:T(4,128)S(1)} %copy.44, f32[30]{0:T(128)S(1)} %iota_add_fusion.5, f32[4,256,256]{2,0,1:T(4,128)S(1)} %copy.45, f32[30,20]{0,1:T(8,128)S(1)} %get-tuple-element.192, ...), kind=kOutput, calls=%fused_computation.19.clone.1 | convolution fusion | flops 385352896 | bytes 3150729 | tf_op jit(solution)/shard_map/while/body/eval_jaxpr/gkab,gjab->kj/dot_general | solution.py:38
  44.1 1.4 %fusion.17 = (f32[4,256,256]{2,1,0:T(8,128)S(1)}, f32[4,256,256]{2,1,0:T(8,128)S(1)}, f32[4,256,256]{2,1,0:T(8,128)S(1)}) fusion(f32[3]{0:T(128)S(1)} %get-tuple-element.207, f32[4,3,256]{2,1,0:T(4,128)S(1)} %get-tuple-element.175, f32[4,3,256]{2,1,0:T(4,128)S(1)} %get-tuple-element.176), kind=kLoop, calls=%fused_computation.15.clone.1 | loop fusion | flops 7077888 | bytes 3170316 | tf_op jit(solution)/shard_map/while/body/eval_jaxpr/reduce_sum | solution.py:25
  45.5 0.5 sqrt_multiply_fusion.2
  46.0 0.7 copy.44
  46.7 0.7 copy.45
  47.4 0.1 copy.43
  47.5 0.3 broadcast_multiply_fusion.4
  47.9 11.9 %fusion.18 = f32[30,20]{0,1:T(8,128)S(1)} fusion(f32[4,256,256]{2,0,1:T(4,128)S(1)} %broadcast_multiply_fusion.4, f32[20]{0:T(128)S(1)} %iota_add_fusion.4, f32[4,256,256]{2,0,1:T(4,128)S(1)} %copy.44, f32[30]{0:T(128)S(1)} %iota_add_fusion.5, f32[4,256,256]{2,0,1:T(4,128)S(1)} %copy.45, f32[30,20]{0,1:T(8,128)S(1)} %get-tuple-element.192, ...), kind=kOutput, calls=%fused_computation.19.clone.1 | convolution fusion | flops 385352896 | bytes 3150729 | tf_op jit(solution)/shard_map/while/body/eval_jaxpr/gkab,gjab->kj/dot_general | solution.py:38
  59.9 1.4 %fusion.17 = (f32[4,256,256]{2,1,0:T(8,128)S(1)}, f32[4,256,256]{2,1,0:T(8,128)S(1)}, f32[4,256,256]{2,1,0:T(8,128)S(1)}) fusion(f32[3]{0:T(128)S(1)} %get-tuple-element.207, f32[4,3,256]{2,1,0:T(4,128)S(1)} %get-tuple-element.175, f32[4,3,256]{2,1,0:T(4,128)S(1)} %get-tuple-element.176), kind=kLoop, calls=%fused_computation.15.clone.1 | loop fusion | flops 7077888 | bytes 3170316 | tf_op jit(solution)/shard_map/while/body/eval_jaxpr/reduce_sum | solution.py:25
  61.3 0.5 sqrt_multiply_fusion.2
  61.8 0.7 copy.44
  62.5 0.7 copy.45
  63.2 0.1 copy.43
  63.3 0.3 broadcast_multiply_fusion.4
  63.7 11.9 %fusion.18 = f32[30,20]{0,1:T(8,128)S(1)} fusion(f32[4,256,256]{2,0,1:T(4,128)S(1)} %broadcast_multiply_fusion.4, f32[20]{0:T(128)S(1)} %iota_add_fusion.4, f32[4,256,256]{2,0,1:T(4,128)S(1)} %copy.44, f32[30]{0:T(128)S(1)} %iota_add_fusion.5, f32[4,256,256]{2,0,1:T(4,128)S(1)} %copy.45, f32[30,20]{0,1:T(8,128)S(1)} %get-tuple-element.192, ...), kind=kOutput, calls=%fused_computation.19.clone.1 | convolution fusion | flops 385352896 | bytes 3150729 | tf_op jit(solution)/shard_map/while/body/eval_jaxpr/gkab,gjab->kj/dot_general | solution.py:38
  75.7 1.4 %fusion.17 = (f32[4,256,256]{2,1,0:T(8,128)S(1)}, f32[4,256,256]{2,1,0:T(8,128)S(1)}, f32[4,256,256]{2,1,0:T(8,128)S(1)}) fusion(f32[3]{0:T(128)S(1)} %get-tuple-element.207, f32[4,3,256]{2,1,0:T(4,128)S(1)} %get-tuple-element.175, f32[4,3,256]{2,1,0:T(4,128)S(1)} %get-tuple-element.176), kind=kLoop, calls=%fused_computation.15.clone.1 | loop fusion | flops 7077888 | bytes 3170316 | tf_op jit(solution)/shard_map/while/body/eval_jaxpr/reduce_sum | solution.py:25
  77.1 0.5 sqrt_multiply_fusion.2
  77.6 0.7 copy.44
  78.3 0.7 copy.45
  79.0 0.1 copy.43
  79.2 0.3 broadcast_multiply_fusion.4
  79.5 11.9 %fusion.18 = f32[30,20]{0,1:T(8,128)S(1)} fusion(f32[4,256,256]{2,0,1:T(4,128)S(1)} %broadcast_multiply_fusion.4, f32[20]{0:T(128)S(1)} %iota_add_fusion.4, f32[4,256,256]{2,0,1:T(4,128)S(1)} %copy.44, f32[30]{0:T(128)S(1)} %iota_add_fusion.5, f32[4,256,256]{2,0,1:T(4,128)S(1)} %copy.45, f32[30,20]{0,1:T(8,128)S(1)} %get-tuple-element.192, ...), kind=kOutput, calls=%fused_computation.19.clone.1 | convolution fusion | flops 385352896 | bytes 3150729 | tf_op jit(solution)/shard_map/while/body/eval_jaxpr/gkab,gjab->kj/dot_general | solution.py:38
  91.5 22.3 %psum.14 = f32[30,20]{0,1:T(8,128)S(1)} all-reduce(f32[30,20]{0,1:T(8,128)S(1)} %get-tuple-element.39), channel_id=1, replica_groups=mesh['gx'=4,'wa'=8] {'wa'}, use_global_device_ids=true, to_apply=%region_5.6 | all-reduce | flops 600 | bytes 4800 | tf_op jit(solution)/shard_map/psum | solution.py:79
  113.8 17.1 %psum.15 = f32[30,20]{0,1:T(8,128)S(1)} all-reduce(f32[30,20]{0,1:T(8,128)S(1)} %broadcast_multiply_fusion.2), channel_id=1, replica_groups=mesh['gx'=4,'wa'=8] {'gx'}, use_global_device_ids=true, to_apply=%region_6.7 | all-reduce | flops 600 | bytes 4800 | tf_op jit(solution)/shard_map/psum | solution.py:80
  130.9 0.6 broadcast_in_dim.24
  131.6 0.6 broadcast_multiply_fusion.1
  (32 shorter events, 0.3 us)
Async XLA Ops:
  0.6 8.8 %copy-start = (f32[16,3,256]{2,0,1:T(8,128)S(1)}, f32[16,3,256]{2,0,1:T(8,128)}, u32[]{:S(2)}) copy-start(f32[16,3,256]{2,0,1:T(8,128)} %param.9) | copy-start | bytes 147460
  0.6 27.5 %copy-start.1 = (f32[3]{0:T(128)S(1)}, f32[3]{0:T(128)}, u32[]{:S(2)}) copy-start(f32[3]{0:T(128)} %constant.46.clone..sunk.3) | copy-start | bytes 40
  3.5 10.0 %all-to-all-start.1 = ((f32[8,2,256]{2,1,0:T(2,128)}), f32[8,2,256]{2,1,0:T(2,128)S(1)}, u32[]{:S(2)}, u32[]{:S(2)}) async-start(f32[8,2,256]{2,1,0:T(2,128)} %reshape.132), calls=%async_computation.1 | async-start | bytes 32768 | tf_op jit(solution)/shard_map/all_to_all | solution.py:53
  13.5 8.2 %all-to-all-start = ((f32[8,2,3,256]{3,1,2,0:T(2,128)}), f32[8,2,3,256]{3,1,2,0:T(2,128)S(1)}, u32[]{:S(2)}, u32[]{:S(2)}) async-start(f32[8,2,3,256]{3,1,2,0:T(2,128)} %copy.31), calls=%async_computation | async-start | bytes 98304 | tf_op jit(solution)/shard_map/all_to_all | solution.py:52
  16.8 6.5 %collective-permute-start.1 = (f32[8,2,256]{2,1,0:T(2,128)S(1)}, f32[8,2,256]{2,1,0:T(2,128)S(1)}, u32[]{:S(2)}, u32[]{:S(2)}) collective-permute-start(f32[8,2,256]{2,1,0:T(2,128)S(1)} %all-to-all-done.1), channel_id=1, source_target_pairs={{0,8},{8,16},{16,24},{24,0},{1,9},{9,17},{17,25},{25,1},{2,10},{10... | collective-permute-start | bytes 49160 | tf_op jit(solution)/shard_map/ppermute | solution.py:15
  21.7 5.9 %collective-permute-start = (f32[8,2,3,256]{3,1,2,0:T(2,128)S(1)}, f32[8,2,3,256]{3,1,2,0:T(2,128)S(1)}, u32[]{:S(2)}, u32[]{:S(2)}) collective-permute-start(f32[8,2,3,256]{3,1,2,0:T(2,128)S(1)} %all-to-all-done), channel_id=1, source_target_pairs={{0,8},{8,16},{16,24},{24,0},{1,9},{9,17},{17,25},{25,1},{2,10},{10... | collective-permute-start | bytes 147464 | tf_op jit(solution)/shard_map/ppermute | solution.py:15
where the time goes:
time: 133 us; the launch traced here: 132 us
  matrix products  47.8 us (36%)
  blocking collectives  39.5 us (30%)
  starting transfers between devices  11.7 us (9%)
  local copies, waits for them, and re-layouts  11.3 us (8%)
  other arithmetic  11.2 us (8%)
  waiting for transfers between devices  8.92 us (7%)
  between operations  1.38 us (1%)
    dot_general x4, matrix products, group_counts(): jnp.einsum('gkab,gjab->kj', s_hat, m_hat, preferred_element_type=jnp.floa...  47.8 us
    psum x1, blocking collectives, per_device(): slab = lax.psum(total, 'wa') * scale  22.3 us
    psum x1, blocking collectives, per_device(): whole = lax.psum(slab, 'gx') / lax.axis_size('gx')  17.1 us
    reduce_sum x4, other arithmetic, group_counts(): jnp.sum(diff * middle, axis=1)  5.74 us
    all_to_all x1, starting transfers between devices, per_device(): lax.all_to_all(send_wgt, 'wa', split_axis=0, concat_axis=0, tiled=True)  5.2 us
    ppermute x2, waiting for transfers between devices, passed_along(): lax.ppermute(shard, axis, [(i, (i + by) % count) for i in range(count)])  3.6 us
    all_to_all x1, starting transfers between devices, per_device(): lax.all_to_all(send_pos, 'wa', split_axis=0, concat_axis=0, tiled=True)  3.35 us
    ppermute x2, starting transfers between devices, passed_along(): lax.ppermute(shard, axis, [(i, (i + by) % count) for i in range(count)])  3.21 us
  transfers between devices with their start and end apart: 4, of which 3 were waited for; matrix products, arithmetic and copies ran while one was open for 2% of the time, Pallas kernels for 0%

commit v1 on v0

--- a/solution.py
+++ b/solution.py
@@ -77,7 +77,7 @@
     total, _ = lax.scan(accumulate, start, items)
     scale = 10.0 * SBINS * MUBINS / (peers * units * block * block)
     slab = lax.psum(total, "wa") * scale
-    whole = lax.psum(slab, "gx") / lax.axis_size("gx")
+    whole = jnp.sum(lax.all_gather(slab, "gx"), axis=0) / lax.axis_size("gx")
     return (slab[None], whole)
 
 

time: 133 us -> 129 us (0.970)
  blocking collectives: 39.5 us -> 35.4 us
    psum x1 -> x0, blocking collectives: 17.1 us -> none  [per_device(): whole = lax.psum(slab, 'gx') / lax.axis_size('gx')]
    all_gather x0 -> x1, blocking collectives: none -> 13.1 us  [per_device(): whole = jnp.sum(lax.all_gather(slab, 'gx'), axis=0) / lax.axis_size('gx')]
where the time goes in v1:
time: 129 us; the launch traced here: 128 us
  matrix products  47.8 us (37%)
  blocking collectives  35.4 us (27%)
  starting transfers between devices  11.7 us (9%)
  local copies, waits for them, and re-layouts  11.3 us (9%)
  other arithmetic  11.2 us (9%)
  waiting for transfers between devices  8.92 us (7%)
  between operations  1.39 us (1%)
    dot_general x4, matrix products, group_counts(): jnp.einsum('gkab,gjab->kj', s_hat, m_hat, preferred_element_type=jnp.floa...  47.8 us
    psum x1, blocking collectives, per_device(): slab = lax.psum(total, 'wa') * scale  22.3 us
    all_gather x1, blocking collectives, per_device(): whole = jnp.sum(lax.all_gather(slab, 'gx'), axis=0) / lax.axis_size('gx')  13.1 us
    reduce_sum x4, other arithmetic, group_counts(): jnp.sum(diff * middle, axis=1)  5.74 us
    all_to_all x1, starting transfers between devices, per_device(): lax.all_to_all(send_wgt, 'wa', split_axis=0, concat_axis=0, tiled=True)  5.2 us
    ppermute x2, waiting for transfers between devices, passed_along(): lax.ppermute(shard, axis, [(i, (i + by) % count) for i in range(count)])  3.6 us
    all_to_all x1, starting transfers between devices, per_device(): lax.all_to_all(send_pos, 'wa', split_axis=0, concat_axis=0, tiled=True)  3.35 us
    ppermute x2, starting transfers between devices, passed_along(): lax.ppermute(shard, axis, [(i, (i + by) % count) for i in range(count)])  3.21 us
  transfers between devices with their start and end apart: 4, of which 3 were waited for; matrix products, arithmetic and copies ran while one was open for 2% of the time, Pallas kernels for 0%

profile of v1, /device:TPU:0, one launch (start us, length us, event | category | flops | bytes accessed | tf_op | source)
XLA Modules:
  0.0 128.1 jit_solution(15230465148569313329)
XLA Ops:
  0.6 0.0 copy-start
  0.6 0.0 copy-start.1
  0.7 0.8 copy.32
  1.4 0.1 reshape_squeeze.3
  1.5 0.8 fusion.12
  2.3 0.6 gather_fusion.2
  2.9 0.6 reshape.132
  3.5 5.2 %all-to-all-start.1 = ((f32[8,2,256]{2,1,0:T(2,128)}), f32[8,2,256]{2,1,0:T(2,128)S(1)}, u32[]{:S(2)}, u32[]{:S(2)}) async-start(f32[8,2,256]{2,1,0:T(2,128)} %reshape.132), calls=%async_computation.1 | async-start | bytes 32768 | tf_op jit(solution)/shard_map/all_to_all | solution.py:53
  8.7 0.7 fusion.14
  9.4 0.0 copy-done
  9.4 0.6 gather_fusion
  10.0 0.6 copy.33
  11.3 2.1 %all-to-all-done.1 = f32[8,2,256]{2,1,0:T(2,128)S(1)} async-done(((f32[8,2,256]{2,1,0:T(2,128)}), f32[8,2,256]{2,1,0:T(2,128)S(1)}, u32[]{:S(2)}, u32[]{:S(2)}) %all-to-all-start.1) | async-done | bytes 16416 | tf_op jit(solution)/shard_map/all_to_all | solution.py:53
  13.5 3.3 %all-to-all-start = ((f32[8,2,3,256]{3,1,2,0:T(2,128)}), f32[8,2,3,256]{3,1,2,0:T(2,128)S(1)}, u32[]{:S(2)}, u32[]{:S(2)}) async-start(f32[8,2,3,256]{3,1,2,0:T(2,128)} %copy.33), calls=%async_computation | async-start | bytes 98304 | tf_op jit(solution)/shard_map/all_to_all | solution.py:52
  16.8 1.6 %collective-permute-start.1 = (f32[8,2,256]{2,1,0:T(2,128)S(1)}, f32[8,2,256]{2,1,0:T(2,128)S(1)}, u32[]{:S(2)}, u32[]{:S(2)}) collective-permute-start(f32[8,2,256]{2,1,0:T(2,128)S(1)} %all-to-all-done.1), channel_id=1, source_target_pairs={{0,8},{8,16},{16,24},{24,0},{1,9},{9,17},{17,25},{25,1},{2,10},{10... | collective-permute-start | bytes 49160 | tf_op jit(solution)/shard_map/ppermute | solution.py:15
  18.5 3.2 %all-to-all-done = f32[8,2,3,256]{3,1,2,0:T(2,128)S(1)} async-done(((f32[8,2,3,256]{3,1,2,0:T(2,128)}), f32[8,2,3,256]{3,1,2,0:T(2,128)S(1)}, u32[]{:S(2)}, u32[]{:S(2)}) %all-to-all-start) | async-done | bytes 49184 | tf_op jit(solution)/shard_map/all_to_all | solution.py:52
  21.7 1.6 %collective-permute-start = (f32[8,2,3,256]{3,1,2,0:T(2,128)S(1)}, f32[8,2,3,256]{3,1,2,0:T(2,128)S(1)}, u32[]{:S(2)}, u32[]{:S(2)}) collective-permute-start(f32[8,2,3,256]{3,1,2,0:T(2,128)S(1)} %all-to-all-done), channel_id=1, source_target_pairs={{0,8},{8,16},{16,24},{24,0},{1,9},{9,17},{17,25},{25,1},{2,10},{10... | collective-permute-start | bytes 147464 | tf_op jit(solution)/shard_map/ppermute | solution.py:15
  23.3 0.1 broadcast_select_fusion
  23.3 0.0 collective-permute-done.1
  23.4 0.6 gather_fusion.3
  24.0 3.6 %collective-permute-done = f32[8,2,3,256]{3,1,2,0:T(2,128)S(1)} collective-permute-done((f32[8,2,3,256]{3,1,2,0:T(2,128)S(1)}, f32[8,2,3,256]{3,1,2,0:T(2,128)S(1)}, u32[]{:S(2)}, u32[]{:S(2)}) %collective-permute-start) | collective-permute-done | bytes 49184 | tf_op jit(solution)/shard_map/ppermute | solution.py:15
  27.6 0.6 gather_fusion.1
  28.2 0.0 copy-done.1
  28.2 63.3 %while.12 = (s32[]{:T(128)}, f32[30,20]{0,1:T(8,128)S(1)}, f32[4,4,3,256]{3,2,1,0:T(4,128)S(1)}, f32[4,4,3,256]{3,2,1,0:T(4,128)S(1)}, f32[4,4,256]{2,1,0:T(4,12...) while((s32[]{:T(128)}, f32[30,20]{0,1:T(8,128)S(1)}, ...), condition=%wide.region_4.5_spmd.clone.clone, body=%wide.region_0.4_spmd.sunk.clone.clone.sunk | while | flops 394265856 | bytes 16889040 | solution.py:77
  28.2 1.4 %fusion.17 = (f32[4,256,256]{2,1,0:T(8,128)S(1)}, f32[4,256,256]{2,1,0:T(8,128)S(1)}, f32[4,256,256]{2,1,0:T(8,128)S(1)}) fusion(f32[3]{0:T(128)S(1)} %get-tuple-element.213, f32[4,3,256]{2,1,0:T(4,128)S(1)} %get-tuple-element.181, f32[4,3,256]{2,1,0:T(4,128)S(1)} %get-tuple-element.182), kind=kLoop, calls=%fused_computation.15.clone.1 | loop fusion | flops 7077888 | bytes 3170316 | tf_op jit(solution)/shard_map/while/body/eval_jaxpr/reduce_sum | solution.py:25
  29.7 0.5 sqrt_multiply_fusion.2
  30.2 0.7 copy.47
  30.8 0.7 copy.48
  31.5 0.1 copy.46
  31.7 0.3 broadcast_multiply_fusion.3
  32.1 11.9 %fusion.18 = f32[30,20]{0,1:T(8,128)S(1)} fusion(f32[4,256,256]{2,0,1:T(4,128)S(1)} %broadcast_multiply_fusion.3, f32[20]{0:T(128)S(1)} %iota_add_fusion.4, f32[4,256,256]{2,0,1:T(4,128)S(1)} %copy.47, f32[30]{0:T(128)S(1)} %iota_add_fusion.5, f32[4,256,256]{2,0,1:T(4,128)S(1)} %copy.48, f32[30,20]{0,1:T(8,128)S(1)} %get-tuple-element.198, ...), kind=kOutput, calls=%fused_computation.19.clone.1 | convolution fusion | flops 385352896 | bytes 3150729 | tf_op jit(solution)/shard_map/while/body/eval_jaxpr/gkab,gjab->kj/dot_general | solution.py:38
  44.1 1.4 %fusion.17 = (f32[4,256,256]{2,1,0:T(8,128)S(1)}, f32[4,256,256]{2,1,0:T(8,128)S(1)}, f32[4,256,256]{2,1,0:T(8,128)S(1)}) fusion(f32[3]{0:T(128)S(1)} %get-tuple-element.213, f32[4,3,256]{2,1,0:T(4,128)S(1)} %get-tuple-element.181, f32[4,3,256]{2,1,0:T(4,128)S(1)} %get-tuple-element.182), kind=kLoop, calls=%fused_computation.15.clone.1 | loop fusion | flops 7077888 | bytes 3170316 | tf_op jit(solution)/shard_map/while/body/eval_jaxpr/reduce_sum | solution.py:25
  45.5 0.5 sqrt_multiply_fusion.2
  46.0 0.7 copy.47
  46.7 0.7 copy.48
  47.4 0.1 copy.46
  47.5 0.3 broadcast_multiply_fusion.3
  47.9 11.9 %fusion.18 = f32[30,20]{0,1:T(8,128)S(1)} fusion(f32[4,256,256]{2,0,1:T(4,128)S(1)} %broadcast_multiply_fusion.3, f32[20]{0:T(128)S(1)} %iota_add_fusion.4, f32[4,256,256]{2,0,1:T(4,128)S(1)} %copy.47, f32[30]{0:T(128)S(1)} %iota_add_fusion.5, f32[4,256,256]{2,0,1:T(4,128)S(1)} %copy.48, f32[30,20]{0,1:T(8,128)S(1)} %get-tuple-element.198, ...), kind=kOutput, calls=%fused_computation.19.clone.1 | convolution fusion | flops 385352896 | bytes 3150729 | tf_op jit(solution)/shard_map/while/body/eval_jaxpr/gkab,gjab->kj/dot_general | solution.py:38
  59.9 1.4 %fusion.17 = (f32[4,256,256]{2,1,0:T(8,128)S(1)}, f32[4,256,256]{2,1,0:T(8,128)S(1)}, f32[4,256,256]{2,1,0:T(8,128)S(1)}) fusion(f32[3]{0:T(128)S(1)} %get-tuple-element.213, f32[4,3,256]{2,1,0:T(4,128)S(1)} %get-tuple-element.181, f32[4,3,256]{2,1,0:T(4,128)S(1)} %get-tuple-element.182), kind=kLoop, calls=%fused_computation.15.clone.1 | loop fusion | flops 7077888 | bytes 3170316 | tf_op jit(solution)/shard_map/while/body/eval_jaxpr/reduce_sum | solution.py:25
  61.3 0.5 sqrt_multiply_fusion.2
  61.8 0.7 copy.47
  62.5 0.7 copy.48
  63.2 0.1 copy.46
  63.3 0.3 broadcast_multiply_fusion.3
  63.7 11.9 %fusion.18 = f32[30,20]{0,1:T(8,128)S(1)} fusion(f32[4,256,256]{2,0,1:T(4,128)S(1)} %broadcast_multiply_fusion.3, f32[20]{0:T(128)S(1)} %iota_add_fusion.4, f32[4,256,256]{2,0,1:T(4,128)S(1)} %copy.47, f32[30]{0:T(128)S(1)} %iota_add_fusion.5, f32[4,256,256]{2,0,1:T(4,128)S(1)} %copy.48, f32[30,20]{0,1:T(8,128)S(1)} %get-tuple-element.198, ...), kind=kOutput, calls=%fused_computation.19.clone.1 | convolution fusion | flops 385352896 | bytes 3150729 | tf_op jit(solution)/shard_map/while/body/eval_jaxpr/gkab,gjab->kj/dot_general | solution.py:38
  75.7 1.4 %fusion.17 = (f32[4,256,256]{2,1,0:T(8,128)S(1)}, f32[4,256,256]{2,1,0:T(8,128)S(1)}, f32[4,256,256]{2,1,0:T(8,128)S(1)}) fusion(f32[3]{0:T(128)S(1)} %get-tuple-element.213, f32[4,3,256]{2,1,0:T(4,128)S(1)} %get-tuple-element.181, f32[4,3,256]{2,1,0:T(4,128)S(1)} %get-tuple-element.182), kind=kLoop, calls=%fused_computation.15.clone.1 | loop fusion | flops 7077888 | bytes 3170316 | tf_op jit(solution)/shard_map/while/body/eval_jaxpr/reduce_sum | solution.py:25
  77.1 0.5 sqrt_multiply_fusion.2
  77.6 0.7 copy.47
  78.3 0.7 copy.48
  79.0 0.1 copy.46
  79.2 0.3 broadcast_multiply_fusion.3
  79.5 11.9 %fusion.18 = f32[30,20]{0,1:T(8,128)S(1)} fusion(f32[4,256,256]{2,0,1:T(4,128)S(1)} %broadcast_multiply_fusion.3, f32[20]{0:T(128)S(1)} %iota_add_fusion.4, f32[4,256,256]{2,0,1:T(4,128)S(1)} %copy.47, f32[30]{0:T(128)S(1)} %iota_add_fusion.5, f32[4,256,256]{2,0,1:T(4,128)S(1)} %copy.48, f32[30,20]{0,1:T(8,128)S(1)} %get-tuple-element.198, ...), kind=kOutput, calls=%fused_computation.19.clone.1 | convolution fusion | flops 385352896 | bytes 3150729 | tf_op jit(solution)/shard_map/while/body/eval_jaxpr/gkab,gjab->kj/dot_general | solution.py:38
  91.5 22.3 %psum.7 = f32[30,20]{0,1:T(8,128)S(1)} all-reduce(f32[30,20]{0,1:T(8,128)S(1)} %get-tuple-element.39), channel_id=1, replica_groups=mesh['gx'=4,'wa'=8] {'wa'}, use_global_device_ids=true, to_apply=%region_5.6 | all-reduce | flops 600 | bytes 4800 | tf_op jit(solution)/shard_map/psum | solution.py:79
  113.8 13.1 %all-gather.1 = f32[4,30,20]{1,2,0:T(8,128)S(1)} all-gather(f32[1,30,20]{1,2,0:T(8,128)S(1)} %multiply_bitcast_fusion), channel_id=2, replica_groups=mesh['gx'=4,'wa'=8] {'gx'}, dimensions={0}, use_global_device_ids=true | all-gather | bytes 12000 | tf_op jit(solution)/shard_map/all_gather | solution.py:80
  126.9 0.6 copy.38
  127.5 0.6 broadcast_multiply_fusion.1
  (33 shorter events, 0.4 us)
Async XLA Ops:
  0.6 8.8 %copy-start = (f32[16,3,256]{2,0,1:T(8,128)S(1)}, f32[16,3,256]{2,0,1:T(8,128)}, u32[]{:S(2)}) copy-start(f32[16,3,256]{2,0,1:T(8,128)} %param.9) | copy-start | bytes 147460
  0.6 27.5 %copy-start.1 = (f32[3]{0:T(128)S(1)}, f32[3]{0:T(128)}, u32[]{:S(2)}) copy-start(f32[3]{0:T(128)} %constant.46.clone..sunk.3) | copy-start | bytes 40
  3.5 10.0 %all-to-all-start.1 = ((f32[8,2,256]{2,1,0:T(2,128)}), f32[8,2,256]{2,1,0:T(2,128)S(1)}, u32[]{:S(2)}, u32[]{:S(2)}) async-start(f32[8,2,256]{2,1,0:T(2,128)} %reshape.132), calls=%async_computation.1 | async-start | bytes 32768 | tf_op jit(solution)/shard_map/all_to_all | solution.py:53
  13.5 8.2 %all-to-all-start = ((f32[8,2,3,256]{3,1,2,0:T(2,128)}), f32[8,2,3,256]{3,1,2,0:T(2,128)S(1)}, u32[]{:S(2)}, u32[]{:S(2)}) async-start(f32[8,2,3,256]{3,1,2,0:T(2,128)} %copy.33), calls=%async_computation | async-start | bytes 98304 | tf_op jit(solution)/shard_map/all_to_all | solution.py:52
  16.8 6.5 %collective-permute-start.1 = (f32[8,2,256]{2,1,0:T(2,128)S(1)}, f32[8,2,256]{2,1,0:T(2,128)S(1)}, u32[]{:S(2)}, u32[]{:S(2)}) collective-permute-start(f32[8,2,256]{2,1,0:T(2,128)S(1)} %all-to-all-done.1), channel_id=1, source_target_pairs={{0,8},{8,16},{16,24},{24,0},{1,9},{9,17},{17,25},{25,1},{2,10},{10... | collective-permute-start | bytes 49160 | tf_op jit(solution)/shard_map/ppermute | solution.py:15
  21.7 5.9 %collective-permute-start = (f32[8,2,3,256]{3,1,2,0:T(2,128)S(1)}, f32[8,2,3,256]{3,1,2,0:T(2,128)S(1)}, u32[]{:S(2)}, u32[]{:S(2)}) collective-permute-start(f32[8,2,3,256]{3,1,2,0:T(2,128)S(1)} %all-to-all-done), channel_id=1, source_target_pairs={{0,8},{8,16},{16,24},{24,0},{1,9},{9,17},{17,25},{25,1},{2,10},{10... | collective-permute-start | bytes 147464 | tf_op jit(solution)/shard_map/ppermute | solution.py:15
